TPU v7x, 8 devices: a whole 2x2x1 slice. The times are simulated.
8 devices in a mesh: dp: 2 (over z, y), tp: 4 (over x, core).
Axes of the slice: x: 2, y: 2, z: 1, core: 2. Of those that a mesh axis runs over, the one named last changes fastest.
Arguments:
- doc_hidden: bfloat16 [64, 16, 2048], P(('dp', 'tp')), parts along dimension 0
- doc_mask: int32 [64, 16], P(('dp', 'tp')), parts along dimension 0
- query_ids: int32 [64, 64], P(('dp', 'tp')), parts along dimension 0
- positive: int32 [64], P(('dp', 'tp')), parts along dimension 0
- tok_weight: float32 [32000], P('tp')
- w_head: bfloat16 [2048, 32000], P(None, 'tp')
- b_head: float32 [32000], P('tp')
Outputs:
- output 1: float32 [2], P('dp'), parts along dimension 0
- output 2: bfloat16 [4096, 32000], P('dp', 'tp'), parts along dimension 0
- output 3: float32 [64000], P(('dp', 'tp')), parts along dimension 0
- output 4: bfloat16 [64, 16, 2048], P(('dp', 'tp')), parts along dimension 0
There are 2 independent parts. A program takes and returns all parts, laid end to end along the dimension named above; an argument that names none is the same for every part.
All inputs are finite; a program needn't handle non-finite values.
Results may differ from a plain program's by a relative error of at most 0.001.
Values are sent between devices in bfloat16 or wider.
A program may use at most 1 GiB of HBM per device.

v0:
```python
import functools

import jax
import jax.numpy as jnp
from jax import lax
from jax.experimental import pallas as pl
from jax.experimental.pallas import tpu as pltpu
from jax.sharding import PartitionSpec as P

REG_COEF = 32.0
MESH = pl.DeviceIdType.MESH
F32 = jnp.float32
BF16 = jnp.bfloat16
VT = 512
LANES = 128
HALF = 256
ROWS = 128
SUB = 64
CHUNKS = 4
QUERIES = 32
NT_DIMS = (((1,), (1,)), ((), ()))
TN_DIMS = (((0,), (0,)), ((), ()))


def dot(a, b):
    return jnp.dot(a, b, preferred_element_type=F32)


def dot_nt(a, b):
    return lax.dot_general(a, b, NT_DIMS, preferred_element_type=F32)


def dot_tn(a, b):
    return lax.dot_general(a, b, TN_DIMS, preferred_element_type=F32)


def iota(shape, axis):
    return lax.broadcasted_iota(jnp.int32, shape, axis)


def one_hot(cond):
    return jnp.where(cond, 1.0, 0.0).astype(BF16)


def split3(x):
    hi = x.astype(BF16)
    rest = x - hi.astype(F32)
    mid = rest.astype(BF16)
    low = (rest - mid.astype(F32)).astype(BF16)
    return hi, mid, low


def log1p_pos(y):
    return jnp.where(y < 5e-4, y * (1.0 - 0.5 * y), jnp.log(1.0 + y))


def head_kernel(
    reg_weight,
    hid_ref, ids_ref, mask_ref, pos_ref, qw_hbm, bias_hbm, w_hbm,
    loss_ref, db_hbm, gt_hbm, hb_hbm, send_hbm, mine_hbm, part_hbm,
    wv, ybuf, hb, land, raw_a, raw_b, g_a, g_b, acc1, acc2, recv1,
    counts, bm, qw_ref, bias_ref, db_ref, mask_row, ids_all, mask_all, pos_all, s_acc, reg_acc, inbox, ds6,
    w_sem, hid_send, hid_recv, fwd_send, fwd_recv, pk_send, pk_recv, s_send, s_recv, acc_send, acc_recv, out_sem, g_sem,
):
    vocab = wv.shape[0]
    hidden = wv.shape[1]
    full = vocab // VT
    tail = vocab - full * VT
    me = lax.axis_index("tp")
    partner = me + 1 - 2 * lax.rem(me, 2)
    other = lax.rem(me + 2, 4)
    diag = lax.rem(partner + 2, 4)
    slots = (me, partner, other, diag)

    def remote(src, dst, ssem, rsem, dev):
        return pltpu.make_async_remote_copy(src, dst, ssem, rsem, device_id={"tp": dev}, device_id_type=MESH)

    def at(t, off=0, size=VT):
        if isinstance(t, int):
            return pl.ds(t * VT + off, size)
        return pl.ds(pl.multiple_of(t * VT + off, SUB), size)

    def cols(t, off=0, size=VT):
        if isinstance(t, int):
            return pl.ds(t * VT + off, size)
        return pl.ds(pl.multiple_of(t * VT + off, LANES), size)

    def w_copy(t, size=VT):
        return pltpu.make_async_copy(w_hbm.at[at(t, 0, size)], wv.at[at(t, 0, size)], w_sem.at[t])

    rows_in = [
        pltpu.make_async_copy(qw_hbm, qw_ref.at[0], out_sem.at[0]),
        pltpu.make_async_copy(bias_hbm, bias_ref.at[0], out_sem.at[1]),
    ]
    for c in rows_in:
        c.start()
    ahead = 6
    for t in range(ahead):
        w_copy(t).start()

    barrier = pltpu.get_barrier_semaphore()
    for peer in slots[1:]:
        pl.semaphore_signal(barrier, inc=1, device_id={"tp": peer}, device_id_type=MESH)
    pl.semaphore_wait(barrier, 3)

    pk_copies = []
    for k in range(3):
        for i, (src, dst) in enumerate(((ids_ref, ids_all), (mask_ref, mask_all), (pos_ref, pos_all))):
            pk_copies.append(remote(src, dst.at[me], pk_send.at[3 * k + i], pk_recv.at[3 * k + i], slots[k + 1]))
    for c in pk_copies:
        c.start()
    near = remote(hid_ref, land.at[0], hid_send.at[CHUNKS], hid_recv.at[CHUNKS], partner)
    near.start()
    step = ROWS // CHUNKS
    far, relay = [], []
    for k in range(CHUNKS):
        part = pl.ds(k * step, step)
        far.append(remote(hid_ref.at[part], land.at[1, part], hid_send.at[k], hid_recv.at[k], other))
        relay.append(remote(land.at[1, part], land.at[2, part], fwd_send.at[k], fwd_recv.at[k], partner))
    for c in far:
        c.start()

    ones = jnp.ones((16, LANES), BF16)
    sub16 = iota((16, VT), 0)

    def bias_columns(t, size):
        parts = [p.astype(F32) for p in split3(bias_ref[:, cols(t, 0, size)])]
        stack = jnp.zeros((16, size), F32)
        for k in range(3):
            stack = jnp.where(sub16[:, :size] == k, parts[k], stack)
        bm[at(t, 0, size)] = dot_tn(stack.astype(BF16), ones)

    def bias_body(t, carry):
        bias_columns(t, VT)
        return carry

    for c in rows_in:
        c.wait()
    lax.fori_loop(0, full, bias_body, 0)
    bias_columns(full, tail)
    ids_all[me] = ids_ref[...]
    mask_all[me] = mask_ref[...]
    pos_all[me] = pos_ref[...]
    for c in pk_copies:
        c.wait_recv()

    lane8 = iota((8, LANES), 1)
    for h in range(2):
        total = None
        for k in range(2):
            mask = mask_all[slots[2 * h + k]].astype(F32).astype(BF16)
            spread = dot(mask, one_hot((iota((16, LANES), 1) >> 4) + 8 == iota((16, LANES), 0)))
            piece = jnp.sum(jnp.where((lane8 & 15) == iota((8, LANES), 0) + 8 * k, spread, 0.0), axis=0, keepdims=True)
            total = piece if total is None else total + piece
        mask_row[h] = jnp.broadcast_to(total, (8, LANES))

    ids = jnp.concatenate([ids_all[g] for g in range(4)], axis=0)
    raw_a[pl.ds(0, LANES), pl.ds(0, LANES)] = jnp.zeros((LANES, LANES), F32)
    raw_a[pl.ds(0, QUERIES), pl.ds(0, 64)] = ids.astype(F32)
    ids_t = jnp.transpose(raw_a[pl.ds(0, LANES), pl.ds(0, LANES)])
    high = (ids - me * vocab) >> 7
    low = (ids_t.astype(jnp.int32) - me * vocab) & 127
    for q in range(QUERIES):
        hot_hi = one_hot(iota((64, 64), 0) == high[q:q + 1])
        hot_lo = one_hot(iota((64, LANES), 1) == low[:64, q:q + 1])
        counts[pl.ds(q, 64, QUERIES), :] = dot(hot_hi, hot_lo)
    s_acc[...] = jnp.zeros_like(s_acc)
    reg_acc[...] = jnp.zeros_like(reg_acc)

    def place(half, sources):
        r, k = iota((HALF, ROWS), 0), iota((HALF, ROWS), 1)
        pick = [one_hot((k == (r & 7) * 16 + (r >> 4)) & (((r >> 3) & 1) == s)) for s in range(2)]
        for c in range(hidden // VT):
            block = pl.ds(c * VT, VT)
            mixed = dot(pick[0], sources[0][:, block]) + dot(pick[1], sources[1][:, block])
            hb[half, :, block] = mixed.astype(BF16)

    near.wait_recv()
    place(0, (hid_ref, land.at[0]))

    def query_rep(t, off, size):
        out = []
        for c in range(-(-size // LANES)):
            width = min(LANES, size - c * LANES)
            block = t * (VT // LANES) + off // LANES + c
            start = block * QUERIES
            if not isinstance(t, int):
                start = pl.multiple_of(start, QUERIES)
            cnt = counts[pl.ds(start, QUERIES)]
            out.append(cnt[:, :width] * qw_ref[:, cols(t, off + c * LANES, width)])
        return jnp.concatenate(out, axis=1) if len(out) > 1 else out[0]

    def mm(t, half, buf, size=VT):
        buf[pl.ds(0, size)] = dot_nt(wv[at(t, 0, size)], hb[half])

    lane_sub = iota((SUB, LANES), 1)

    def ep(t, half, buf, size=VT):
        mask = mask_row[half, 0:1]
        for r in range(size // SUB):
            rows = pl.ds(r * SUB, SUB)
            here = at(t, r * SUB, SUB)
            col = bm[here]
            bias = col if half == 0 else jnp.broadcast_to(col[:, 0:1], (SUB, LANES))
            acc = None
            for b in range(2):
                y = jnp.maximum(buf[rows, pl.ds(b * LANES, LANES)] + bias, 0.0)
                if b == 1:
                    y = y * mask
                ybuf[here, pl.ds(half * HALF + b * LANES, LANES)] = y
                act = log1p_pos(y)
                acc = act if acc is None else acc + act
            buf[rows, pl.ds(0, LANES)] = acc
            total = jnp.sum(acc, axis=1, keepdims=True)
            if half == 0:
                bm[here] = jnp.where(lane_sub < 64, col, total)
            else:
                mean = jnp.broadcast_to((total + col[:, 64:65]) * (1.0 / 32.0), (SUB, LANES))
                bm[here] = mean
                square = mean * mean
                reg_acc[...] += jnp.sum(square.reshape(SUB // 8, 8, LANES), axis=0)
        for off in range(0, size, HALF):
            depth = min(HALF, size - off)
            rq = split3(query_rep(t, off, depth))
            act = split3(buf[pl.ds(off, depth), pl.ds(0, LANES)])
            s_acc[half] += dot(jnp.concatenate(rq, axis=0), act[0])
            s_acc[half, pl.ds(0, 64)] += dot(jnp.concatenate(rq[:2], axis=0), act[1])
            s_acc[half, pl.ds(0, 32)] += dot(rq[0], act[2])

    def forward(half, tick):
        first = half == 0
        if first:
            w_copy(0).wait()
        mm(0, half, raw_a)

        def body(i, carry):
            t = 2 * i
            if first:
                for u in range(2):
                    @pl.when(t + u + ahead < full)
                    def _():
                        w_copy(t + u + ahead).start()
                @pl.when(i == (full - ahead) // 2)
                def _():
                    w_copy(full, tail).start()
                w_copy(t + 1).wait()
            mm(t + 1, half, raw_b)
            ep(t, half, raw_a)
            if first:
                w_copy(t + 2).wait()
            mm(t + 2, half, raw_a)
            ep(t + 1, half, raw_b)
            tick(i)
            return carry

        lax.fori_loop(0, (full - 1) // 2, body, 0)
        if first:
            w_copy(full, tail).wait()
        mm(full, half, raw_b, tail)
        ep(full - 1, half, raw_a)
        ep(full, half, raw_b, tail)

    def relay_tick(i):
        for k, when in enumerate((0, 2, 4)):
            @pl.when(i == when)
            def _():
                far[k].wait_recv()
                relay[k].start()

    forward(0, relay_tick)
    far[CHUNKS - 1].wait_recv()
    relay[CHUNKS - 1].start()
    for c in relay:
        c.wait_recv()
    place(1, (land.at[1], land.at[2]))
    hb_out = pltpu.make_async_copy(hb, hb_hbm, out_sem.at[3])
    hb_out.start()
    forward(1, lambda i: None)

    def doc_lane(half):
        k = iota((LANES, LANES), 0)
        owner = jnp.where(((k >> 3) & 1) == 0, slots[2 * half], slots[2 * half + 1])
        return one_hot(iota((LANES, LANES), 1) == owner * 8 + (k & 7))

    scores = None
    for h in range(2):
        mine = s_acc[h, pl.ds(0, 32)] + s_acc[h, pl.ds(32, 32)] + s_acc[h, pl.ds(64, 32)]
        moved = dot(jnp.concatenate(split3(mine), axis=0), doc_lane(h))
        moved = moved[0:32] + moved[32:64] + moved[64:96]
        scores = moved if scores is None else scores + moved
    inbox[me, pl.ds(0, 32)] = scores
    inbox[me, pl.ds(32, 8)] = jnp.broadcast_to(jnp.sum(reg_acc[...], axis=0, keepdims=True), (8, LANES))
    s_copies = [remote(inbox.at[me], inbox.at[me], s_send.at[k], s_recv.at[k], slots[k + 1]) for k in range(3)]
    for c in s_copies:
        c.start()
    for c in s_copies:
        c.wait_recv()
    st = inbox[0] + inbox[1] + inbox[2] + inbox[3]
    lane = iota((32, LANES), 1)
    live = lane < 32
    score = jnp.where(live, st[0:32], -3.0e38)
    diagonal = iota((8, 8), 0) == iota((8, 8), 1)
    pos = jnp.concatenate(
        [jnp.sum(jnp.where(diagonal, pos_all[g].astype(F32), 0.0), axis=1, keepdims=True) for g in range(4)], axis=0
    ).astype(jnp.int32)
    onehot = jnp.where(lane == pos, 1.0, 0.0)
    top = jnp.max(score, axis=1, keepdims=True)
    expo = jnp.where(live, jnp.exp(score - top), 0.0)
    norm = jnp.sum(expo, axis=1, keepdims=True)
    per_query = top + jnp.log(norm) - jnp.sum(jnp.where(live, score, 0.0) * onehot, axis=1, keepdims=True)
    loss = jnp.sum(per_query, axis=0, keepdims=True) * (1.0 / 32.0) + st[32:33] * reg_weight
    loss_ref[...] = loss
    d_scores = split3(jnp.where(live, expo / norm - onehot, 0.0) * (1.0 / 32.0))
    for b, h in enumerate((1, 0)):
        lanes = [dot_nt(p, doc_lane(h)).astype(BF16) for p in d_scores]
        for k, p in enumerate((0, 1, 0, 2, 1, 0)):
            ds6[pl.ds(k * 32, 32), pl.ds(b * LANES, LANES)] = lanes[p]

    def g_copy(t, half, buf, k, size=VT):
        return pltpu.make_async_copy(
            buf.at[pl.ds(0, size)], gt_hbm.at[at(t, 0, size), pl.ds(half * HALF, HALF)], g_sem.at[k]
        )

    def grad(t, half, buf, k, size=VT):
        if half == 1:
            hi, mid, lo = split3(query_rep(t, 0, size))
            raw_a[pl.ds(0, size)] = dot_tn(jnp.concatenate([hi, hi, mid, hi, mid, lo], axis=0), ds6[...])
        for r in range(size // SUB):
            rows = pl.ds(r * SUB, SUB)
            here = at(t, r * SUB, SUB)
            d_rep = bm[here]
            if half == 1:
                reg = d_rep * (2.0 * reg_weight / 32.0)
                d_rep = raw_a[rows, pl.ds(0, LANES)] + reg
                bm[here] = raw_a[rows, pl.ds(LANES, LANES)] + reg
            total = None
            for b in range(2):
                y = ybuf[here, pl.ds(half * HALF + b * LANES, LANES)]
                d = jnp.where(y > 0.0, d_rep * (1.0 / (1.0 + y)), 0.0)
                total = d if total is None else total + d
                buf[rows, pl.ds(b * LANES, LANES)] = d.astype(BF16)
            raw_b[rows, pl.ds(0, LANES)] = total
        g_copy(t, half, buf, k, size).start()
        for off in range(0, size, LANES):
            width = min(LANES, size - off)
            row = jnp.sum(jnp.transpose(raw_b[pl.ds(off, LANES), pl.ds(0, LANES)]), axis=0, keepdims=True)[:, :width]
            if half == 1:
                db_ref[:, cols(t, off, width)] = row
            else:
                db_ref[:, cols(t, off, width)] += row

    def mm_t(t, buf, acc, size=VT):
        acc[...] += dot_tn(buf[pl.ds(0, size)], wv[at(t, 0, size)]).reshape(acc.shape)

    def backward(half, acc, tick):
        acc[...] = jnp.zeros_like(acc)
        grad(0, half, g_a, 0)

        def body(i, carry):
            t = 2 * i

            @pl.when(i > 0)
            def _():
                g_copy(t - 1, half, g_b, 1).wait()
            grad(t + 1, half, g_b, 1)
            mm_t(t, g_a, acc)
            g_copy(t, half, g_a, 0).wait()
            grad(t + 2, half, g_a, 0)
            mm_t(t + 1, g_b, acc)
            tick(i)
            return carry

        lax.fori_loop(0, (full - 1) // 2, body, 0)
        g_copy(full - 2, half, g_b, 1).wait()
        mm_t(full - 1, g_a, acc)
        grad(full, half, g_b, 1, tail)
        mm_t(full, g_b, acc, tail)
        g_copy(full - 1, half, g_a, 0).wait()
        g_copy(full, half, g_b, 1, tail).wait()

    backward(1, acc1, lambda i: None)
    swap = remote(acc1.at[:, pl.ds(8, 8)], recv1, acc_send, acc_recv, partner)
    swap.start()
    outs = [
        pltpu.make_async_copy(acc1.at[:, pl.ds(0, 8)], send_hbm, out_sem.at[0]),
        pltpu.make_async_copy(acc2.at[:, pl.ds(0, 8)], mine_hbm, out_sem.at[1]),
        pltpu.make_async_copy(acc2.at[:, pl.ds(8, 8)], part_hbm, out_sem.at[2]),
        pltpu.make_async_copy(db_ref.at[0], db_hbm, out_sem.at[4]),
    ]

    def swap_tick(i):
        @pl.when(i == 4)
        def _():
            swap.wait_recv()
            acc1[:, pl.ds(0, 8)] += recv1[...]
            outs[0].start()

    backward(0, acc2, swap_tick)
    outs[1].start()
    outs[2].start()
    outs[3].start()
    for c in outs:
        c.wait()
    hb_out.wait()
    swap.wait_send()
    near.wait_send()
    for c in pk_copies + far + relay + s_copies:
        c.wait_send()


def weight_kernel(gt_ref, hb_ref, out_ref):
    out_ref[...] = dot(gt_ref[...], hb_ref[...]).astype(BF16)


def finish_kernel(mine_ref, part_ref, far_ref, out_ref):
    total = ((mine_ref[...] + part_ref[...]) + far_ref[...]).astype(BF16)
    r, k = iota((ROWS, ROWS), 0), iota((ROWS, ROWS), 1)
    out_ref[...] = dot(one_hot(k == (r & 15) * 8 + (r >> 4)), total).astype(BF16)


def solution(mesh):
    group_size = mesh.shape['tp']
    row_spec = P(('dp', 'tp'))

    def local_step(doc_hidden, doc_mask, query_ids, positive, tok_weight, w_head, b_head):
        docs, doc_len, hidden = doc_hidden.shape
        vocab = w_head.shape[1]
        reg_weight = REG_COEF / (vocab * group_size * doc_len * doc_len)
        tiles = -(-vocab // VT)
        vmem = pl.BlockSpec(memory_space=pltpu.VMEM)
        hbm = pl.BlockSpec(memory_space=pl.ANY)
        dma = pltpu.SemaphoreType.DMA
        block = jax.ShapeDtypeStruct((16, 8, hidden), F32)
        loss, db, gt, hb, send, mine, part = pl.pallas_call(
            functools.partial(head_kernel, reg_weight),
            out_shape=(
                jax.ShapeDtypeStruct((1, LANES), F32),
                jax.ShapeDtypeStruct((vocab,), F32),
                jax.ShapeDtypeStruct((vocab, 2 * HALF), BF16),
                jax.ShapeDtypeStruct((2, HALF, hidden), BF16),
                block, block, block,
            ),
            in_specs=[vmem, vmem, vmem, vmem, hbm, hbm, hbm],
            out_specs=(vmem, hbm, hbm, hbm, hbm, hbm, hbm),
            scratch_shapes=[
                pltpu.VMEM((vocab, hidden), BF16),
                pltpu.VMEM((vocab, 2 * HALF), F32),
                pltpu.VMEM((2, HALF, hidden), BF16),
                pltpu.VMEM((3, ROWS, hidden), BF16),
                pltpu.VMEM((VT, HALF), F32),
                pltpu.VMEM((VT, HALF), F32),
                pltpu.VMEM((VT, HALF), BF16),
                pltpu.VMEM((VT, HALF), BF16),
                pltpu.VMEM((16, 16, hidden), F32),
                pltpu.VMEM((16, 16, hidden), F32),
                pltpu.VMEM((16, 8, hidden), F32),
                pltpu.VMEM((64 * QUERIES, LANES), F32),
                pltpu.VMEM((vocab, LANES), F32),
                pltpu.VMEM((1, vocab), F32),
                pltpu.VMEM((1, vocab), F32),
                pltpu.VMEM((1, vocab), F32),
                pltpu.VMEM((2, 8, LANES), F32),
                pltpu.VMEM((4, 8, 64), jnp.int32),
                pltpu.VMEM((4, 8, 16), jnp.int32),
                pltpu.VMEM((4, 1, 8), jnp.int32),
                pltpu.VMEM((2, 96, LANES), F32),
                pltpu.VMEM((8, LANES), F32),
                pltpu.VMEM((4, 40, LANES), F32),
                pltpu.VMEM((192, HALF), BF16),
                dma((tiles,)), dma((CHUNKS + 1,)), dma((CHUNKS + 1,)), dma((CHUNKS,)), dma((CHUNKS,)),
                dma((9,)), dma((9,)), dma((3,)), dma((3,)), dma, dma, dma((5,)), dma((2,)),
            ],
            compiler_params=pltpu.CompilerParams(
                collective_id=0, has_side_effects=True, vmem_limit_bytes=67_043_328
            ),
            name='head',
        )(
            doc_hidden.reshape(docs * doc_len, hidden), query_ids, doc_mask, positive.reshape(1, 8),
            tok_weight, b_head, w_head.T,
        )

        cross = [(k, (k + 2) % 4) for k in range(4)]
        swap = [(k, k ^ 1) for k in range(4)]
        rows = (docs * doc_len, hidden)
        far = lax.ppermute(send.reshape(rows), 'tp', cross)
        near = lax.ppermute(part.reshape(rows), 'tp', swap)
        step = 800
        d_weight = pl.pallas_call(
            weight_kernel,
            grid=(vocab // step,),
            out_shape=jax.ShapeDtypeStruct((vocab, hidden), BF16),
            in_specs=[
                pl.BlockSpec((step, 2 * HALF), lambda i: (i, 0)),
                pl.BlockSpec((2 * HALF, hidden), lambda i: (0, 0)),
            ],
            out_specs=pl.BlockSpec((step, hidden), lambda i: (i, 0)),
            cost_estimate=pl.CostEstimate(
                flops=2 * hidden * 2 * HALF * vocab, bytes_accessed=50_000_000, transcendentals=0
            ),
            compiler_params=pltpu.CompilerParams(vmem_limit_bytes=67_043_328),
            name='dweight',
        )(gt, hb.reshape(2 * HALF, hidden))
        d_hidden = pl.pallas_call(
            finish_kernel,
            grid=(4,),
            out_shape=jax.ShapeDtypeStruct(rows, BF16),
            in_specs=[pl.BlockSpec((ROWS, hidden // 4), lambda i: (0, i))] * 3,
            out_specs=pl.BlockSpec((ROWS, hidden // 4), lambda i: (0, i)),
            name='finish',
        )(mine.reshape(rows), near, far)
        return loss[0, :1], d_weight.T, db, d_hidden.reshape(docs, doc_len, hidden)

    return jax.shard_map(
        local_step,
        mesh=mesh,
        in_specs=(row_spec, row_spec, row_spec, row_spec, P('tp'), P(None, 'tp'), P('tp')),
        out_specs=(P('dp'), P('dp', 'tp'), row_spec, row_spec),
        check_vma=False,
    )
```

profile of v0, /device:TPU:0, one launch (start us, length us, event | category | flops | bytes accessed | tf_op | source)
XLA Modules:
  0.0 116.4 jit_solution(9317721047903656674)
XLA Ops:
  0.6 83.1 %head.1 = (f32[1,128]{1,0:T(1,128)}, f32[8000]{0:T(1024)}, bf16[8000,512]{1,0:T(8,128)(2,1)}, bf16[2,256,2048]{2,1,0:T(8,128)(2,1)}, f32[16,8,2048]{2,1,0:T(8,12...) custom-call(bf16[128,2048]{1,0:T(8,128)(2,1)} %bitcast.13, s32[8,64]{1,0:T(8,128)} %ids_ref.1, s32[8,16]{1,0:T(8,128)} %mask_ref.1, ...), custom_call_target="tpu_custom_call" | custom-call | tf_op jit(solution)/shard_map/head/pallas_call | solution.py:434
  83.8 0.1 collective-permute-start
  83.9 0.0 collective-permute-start.1
  83.9 22.3 %dweight.1 = bf16[8000,2048]{1,0:T(8,128)(2,1)} custom-call(bf16[8000,512]{1,0:T(8,128)(2,1)} %get-tuple-element.12.gt_ref, bf16[512,2048]{1,0:T(8,128)(2,1)} %bitcast.16), custom_call_target="tpu_custom_call" | custom-call | flops 16777216000 | bytes 50000000 | tf_op jit(solution)/shard_map/dweight/pallas_call | solution.py:488
  106.2 0.0 collective-permute-done.part_ref
  106.2 3.1 %collective-permute-done.1.far_ref = f32[128,2048]{1,0:T(8,128)} collective-permute-done((f32[128,2048]{1,0:T(8,128)}, f32[128,2048]{1,0:T(8,128)}, u32[]{:S(2)}, u32[]{:S(2)}) %collective-permute-start.1) | collective-permute-done | bytes 1048608 | tf_op jit(solution)/shard_map/ppermute | solution.py:485
  109.4 4.0 %finish.1 = bf16[128,2048]{1,0:T(8,128)(2,1)} custom-call(f32[128,2048]{1,0:T(8,128)} %bitcast.12, f32[128,2048]{1,0:T(8,128)} %collective-permute-done.part_ref, f32[128,2048]{1,0:T(8,128)} %collective-permute-done.1.far_ref), custom_call_target="tpu_custom_call" | custom-call | tf_op jit(solution)/shard_map/finish/pallas_call | solution.py:503
  113.9 1.4 %copy.14 = f32[8000]{0:T(1024)} copy(f32[8000]{0:T(1024)} %get-tuple-element.24) | data formatting | bytes 64000
Async XLA Ops:
  83.8 22.5 %collective-permute-start = (f32[128,2048]{1,0:T(8,128)}, f32[128,2048]{1,0:T(8,128)}, u32[]{:S(2)}, u32[]{:S(2)}) collective-permute-start(f32[128,2048]{1,0:T(8,128)} %bitcast.18), channel_id=1, source_target_pairs={{0,1},{1,0},{2,3},{3,2},{4,5},{5,4},{6,7},{7,6}} | collective-permute-start | bytes 3145736 | tf_op jit(solution)/shard_map/ppermute | solution.py:486
  83.9 25.5 %collective-permute-start.1 = (f32[128,2048]{1,0:T(8,128)}, f32[128,2048]{1,0:T(8,128)}, u32[]{:S(2)}, u32[]{:S(2)}) collective-permute-start(f32[128,2048]{1,0:T(8,128)} %bitcast.17), channel_id=1, source_target_pairs={{0,2},{1,3},{2,0},{3,1},{4,6},{5,7},{6,4},{7,5}} | collective-permute-start | bytes 3145736 | tf_op jit(solution)/shard_map/ppermute | solution.py:485
where the time goes:
time: 117 us; the launch traced here: 116 us
  Pallas kernels  109 us (93%)
  waiting for transfers between devices  3.12 us (3%)
  between operations  2.35 us (2%)
  local copies, waits for them, and re-layouts  1.38 us (1%)
    pallas_call x1, Pallas kernels, local_step(): pl.pallas_call(functools.partial(head_kernel, reg_weight), out_shape=(jax...  83.1 us
    pallas_call x1, Pallas kernels, local_step(): pl.pallas_call(weight_kernel, grid=(vocab // step,), out_shape=jax.ShapeD...  22.3 us
    pallas_call x1, Pallas kernels, local_step(): pl.pallas_call(finish_kernel, grid=(4,), out_shape=jax.ShapeDtypeStruct(r...  3.98 us
    ppermute x1, waiting for transfers between devices, local_step(): far = lax.ppermute(send.reshape(rows), 'tp', cross)  3.12 us
  transfers between devices with their start and end apart: 2, of which 1 were waited for; matrix products, arithmetic and copies ran while one was open for 0% of the time, Pallas kernels for 19%

commit v1 on v0

--- a/solution.py
+++ b/solution.py
@@ -17,6 +17,8 @@
 ROWS = 128
 SUB = 64
 CHUNKS = 4
+MM_ROWS = 256
+MM_COLS = 512
 QUERIES = 32
 NT_DIMS = (((1,), (1,)), ((), ()))
 TN_DIMS = (((0,), (0,)), ((), ()))
@@ -54,12 +56,24 @@
     return jnp.where(y < 5e-4, y * (1.0 - 0.5 * y), jnp.log(1.0 + y))
 
 
+def weave(first, second):
+    count = max(len(first), 1)
+    done = 0
+    for k in range(count):
+        if first:
+            first[k]()
+        upto = -(-len(second) * (k + 1) // count)
+        for piece in second[done:upto]:
+            piece()
+        done = upto
+
+
 def head_kernel(
     reg_weight,
     hid_ref, ids_ref, mask_ref, pos_ref, qw_hbm, bias_hbm, w_hbm,
-    loss_ref, db_hbm, gt_hbm, hb_hbm, send_hbm, mine_hbm, part_hbm,
+    loss_ref, db_ref, gt_hbm, hb_hbm, send_hbm, mine_hbm, part_hbm,
     wv, ybuf, hb, land, raw_a, raw_b, g_a, g_b, acc1, acc2, recv1,
-    counts, bm, qw_ref, bias_ref, db_ref, mask_row, ids_all, mask_all, pos_all, s_acc, reg_acc, inbox, ds6,
+    counts, bm, qw_ref, bias_ref, mask_row, ids_all, mask_all, pos_all, s_acc, reg_acc, inbox, ds6,
     w_sem, hid_send, hid_recv, fwd_send, fwd_recv, pk_send, pk_recv, s_send, s_recv, acc_send, acc_recv, out_sem, g_sem,
 ):
     vocab = wv.shape[0]
@@ -94,7 +108,7 @@
     ]
     for c in rows_in:
         c.start()
-    ahead = 6
+    ahead = 4
     for t in range(ahead):
         w_copy(t).start()
 
@@ -134,10 +148,6 @@
         bias_columns(t, VT)
         return carry
 
-    for c in rows_in:
-        c.wait()
-    lax.fori_loop(0, full, bias_body, 0)
-    bias_columns(full, tail)
     ids_all[me] = ids_ref[...]
     mask_all[me] = mask_ref[...]
     pos_all[me] = pos_ref[...]
@@ -175,6 +185,10 @@
             mixed = dot(pick[0], sources[0][:, block]) + dot(pick[1], sources[1][:, block])
             hb[half, :, block] = mixed.astype(BF16)
 
+    for c in rows_in:
+        c.wait()
+    lax.fori_loop(0, full, bias_body, 0)
+    bias_columns(full, tail)
     near.wait_recv()
     place(0, (hid_ref, land.at[0]))
 
@@ -191,47 +205,63 @@
         return jnp.concatenate(out, axis=1) if len(out) > 1 else out[0]
 
     def mm(t, half, buf, size=VT):
-        buf[pl.ds(0, size)] = dot_nt(wv[at(t, 0, size)], hb[half])
+        def piece(off, depth):
+            def run():
+                buf[pl.ds(off, depth)] = dot_nt(wv[at(t, off, depth)], hb[half])
+            return run
+        return [piece(off, min(MM_ROWS, size - off)) for off in range(0, size, MM_ROWS)]
 
     lane_sub = iota((SUB, LANES), 1)
 
     def ep(t, half, buf, size=VT):
-        mask = mask_row[half, 0:1]
-        for r in range(size // SUB):
-            rows = pl.ds(r * SUB, SUB)
-            here = at(t, r * SUB, SUB)
-            col = bm[here]
-            bias = col if half == 0 else jnp.broadcast_to(col[:, 0:1], (SUB, LANES))
-            acc = None
-            for b in range(2):
-                y = jnp.maximum(buf[rows, pl.ds(b * LANES, LANES)] + bias, 0.0)
-                if b == 1:
-                    y = y * mask
-                ybuf[here, pl.ds(half * HALF + b * LANES, LANES)] = y
-                act = log1p_pos(y)
-                acc = act if acc is None else acc + act
-            buf[rows, pl.ds(0, LANES)] = acc
-            total = jnp.sum(acc, axis=1, keepdims=True)
-            if half == 0:
-                bm[here] = jnp.where(lane_sub < 64, col, total)
-            else:
-                mean = jnp.broadcast_to((total + col[:, 64:65]) * (1.0 / 32.0), (SUB, LANES))
-                bm[here] = mean
-                square = mean * mean
-                reg_acc[...] += jnp.sum(square.reshape(SUB // 8, 8, LANES), axis=0)
+        def rows_piece(r):
+            def run():
+                mask = mask_row[half, 0:1]
+                rows = pl.ds(r * SUB, SUB)
+                here = at(t, r * SUB, SUB)
+                col = bm[here]
+                bias = col if half == 0 else jnp.broadcast_to(col[:, 0:1], (SUB, LANES))
+                acc = None
+                for b in range(2):
+                    y = jnp.maximum(buf[rows, pl.ds(b * LANES, LANES)] + bias, 0.0)
+                    if b == 1:
+                        y = y * mask
+                    ybuf[here, pl.ds(half * HALF + b * LANES, LANES)] = y
+                    act = log1p_pos(y)
+                    acc = act if acc is None else acc + act
+                buf[rows, pl.ds(0, LANES)] = acc
+                total = jnp.sum(acc, axis=1, keepdims=True)
+                if half == 0:
+                    bm[here] = jnp.where(lane_sub < 64, col, total)
+                else:
+                    mean = jnp.broadcast_to((total + col[:, 64:65]) * (1.0 / 32.0), (SUB, LANES))
+                    bm[here] = mean
+                    square = mean * mean
+                    reg_acc[...] += jnp.sum(square.reshape(SUB // 8, 8, LANES), axis=0)
+            return run
+
+        def score_piece(off):
+            def run():
+                depth = min(HALF, size - off)
+                rq = split3(query_rep(t, off, depth))
+                act = split3(buf[pl.ds(off, depth), pl.ds(0, LANES)])
+                s_acc[half] += dot(jnp.concatenate(rq, axis=0), act[0])
+                s_acc[half, pl.ds(0, 64)] += dot(jnp.concatenate(rq[:2], axis=0), act[1])
+                s_acc[half, pl.ds(0, 32)] += dot(rq[0], act[2])
+            return run
+
+        out = []
         for off in range(0, size, HALF):
-            depth = min(HALF, size - off)
-            rq = split3(query_rep(t, off, depth))
-            act = split3(buf[pl.ds(off, depth), pl.ds(0, LANES)])
-            s_acc[half] += dot(jnp.concatenate(rq, axis=0), act[0])
-            s_acc[half, pl.ds(0, 64)] += dot(jnp.concatenate(rq[:2], axis=0), act[1])
-            s_acc[half, pl.ds(0, 32)] += dot(rq[0], act[2])
+            for r in range(off // SUB, min(off + HALF, size) // SUB):
+                out.append(rows_piece(r))
+            out.append(score_piece(off))
+        return out
 
     def forward(half, tick):
         first = half == 0
         if first:
             w_copy(0).wait()
-        mm(0, half, raw_a)
+        weave(mm(0, half, raw_a), [])
 
         def body(i, carry):
             t = 2 * i
@@ -244,21 +274,18 @@
                 def _():
                     w_copy(full, tail).start()
                 w_copy(t + 1).wait()
-            mm(t + 1, half, raw_b)
-            ep(t, half, raw_a)
+            weave(mm(t + 1, half, raw_b), ep(t, half, raw_a))
             if first:
                 w_copy(t + 2).wait()
-            mm(t + 2, half, raw_a)
-            ep(t + 1, half, raw_b)
+            weave(mm(t + 2, half, raw_a), ep(t + 1, half, raw_b))
             tick(i)
             return carry
 
         lax.fori_loop(0, (full - 1) // 2, body, 0)
         if first:
             w_copy(full, tail).wait()
-        mm(full, half, raw_b, tail)
-        ep(full - 1, half, raw_a)
-        ep(full, half, raw_b, tail)
+        weave(mm(full, half, raw_b, tail), ep(full - 1, half, raw_a))
+        weave([], ep(full, half, raw_b, tail))
 
     def relay_tick(i):
         for k, when in enumerate((0, 2, 4)):
@@ -322,39 +349,59 @@
         )
 
     def grad(t, half, buf, k, size=VT):
-        if half == 1:
-            hi, mid, lo = split3(query_rep(t, 0, size))
-            raw_a[pl.ds(0, size)] = dot_tn(jnp.concatenate([hi, hi, mid, hi, mid, lo], axis=0), ds6[...])
-        for r in range(size // SUB):
-            rows = pl.ds(r * SUB, SUB)
-            here = at(t, r * SUB, SUB)
-            d_rep = bm[here]
+        def setup(off):
+            def run():
+                depth = min(HALF, size - off)
+                hi, mid, lo = split3(query_rep(t, off, depth))
+                raw_a[pl.ds(off, depth)] = dot_tn(jnp.concatenate([hi, hi, mid, hi, mid, lo], axis=0), ds6[...])
+            return run
+
+        def rows_piece(r):
+            def run():
+                rows = pl.ds(r * SUB, SUB)
+                here = at(t, r * SUB, SUB)
+                d_rep = bm[here]
+                if half == 1:
+                    reg = d_rep * (2.0 * reg_weight / 32.0)
+                    d_rep = raw_a[rows, pl.ds(0, LANES)] + reg
+                    bm[here] = raw_a[rows, pl.ds(LANES, LANES)] + reg
+                total = None
+                for b in range(2):
+                    y = ybuf[here, pl.ds(half * HALF + b * LANES, LANES)]
+                    d = jnp.where(y > 0.0, d_rep * (1.0 / (1.0 + y)), 0.0)
+                    total = d if total is None else total + d
+                    buf[rows, pl.ds(b * LANES, LANES)] = d.astype(BF16)
+                raw_b[rows, pl.ds(0, LANES)] = total
+            return run
+
+        def finish():
+            g_copy(t, half, buf, k, size).start()
+            for off in range(0, size, LANES):
+                width = min(LANES, size - off)
+                row = jnp.sum(jnp.transpose(raw_b[pl.ds(off, LANES), pl.ds(0, LANES)]), axis=0, keepdims=True)[:, :width]
+                if half == 1:
+                    db_ref[:, cols(t, off, width)] = row
+                else:
+                    db_ref[:, cols(t, off, width)] += row
+
+        out = []
+        for off in range(0, size, HALF):
             if half == 1:
-                reg = d_rep * (2.0 * reg_weight / 32.0)
-                d_rep = raw_a[rows, pl.ds(0, LANES)] + reg
-                bm[here] = raw_a[rows, pl.ds(LANES, LANES)] + reg
-            total = None
-            for b in range(2):
-                y = ybuf[here, pl.ds(half * HALF + b * LANES, LANES)]
-                d = jnp.where(y > 0.0, d_rep * (1.0 / (1.0 + y)), 0.0)
-                total = d if total is None else total + d
-                buf[rows, pl.ds(b * LANES, LANES)] = d.astype(BF16)
-            raw_b[rows, pl.ds(0, LANES)] = total
-        g_copy(t, half, buf, k, size).start()
-        for off in range(0, size, LANES):
-            width = min(LANES, size - off)
-            row = jnp.sum(jnp.transpose(raw_b[pl.ds(off, LANES), pl.ds(0, LANES)]), axis=0, keepdims=True)[:, :width]
-            if half == 1:
-                db_ref[:, cols(t, off, width)] = row
-            else:
-                db_ref[:, cols(t, off, width)] += row
+                out.append(setup(off))
+            out += [rows_piece(r) for r in range(off // SUB, min(off + HALF, size) // SUB)]
+        return out + [finish]
 
     def mm_t(t, buf, acc, size=VT):
-        acc[...] += dot_tn(buf[pl.ds(0, size)], wv[at(t, 0, size)]).reshape(acc.shape)
+        def piece(n):
+            def run():
+                block = pl.ds(n * MM_COLS, MM_COLS)
+                acc[:, :, block] += dot_tn(buf[pl.ds(0, size)], wv[at(t, 0, size), block]).reshape(16, 16, MM_COLS)
+            return run
+        return [piece(n) for n in range(hidden // MM_COLS)]
 
     def backward(half, acc, tick):
         acc[...] = jnp.zeros_like(acc)
-        grad(0, half, g_a, 0)
+        weave([], grad(0, half, g_a, 0))
 
         def body(i, carry):
             t = 2 * i
@@ -362,19 +409,16 @@
             @pl.when(i > 0)
             def _():
                 g_copy(t - 1, half, g_b, 1).wait()
-            grad(t + 1, half, g_b, 1)
-            mm_t(t, g_a, acc)
+            weave(mm_t(t, g_a, acc), grad(t + 1, half, g_b, 1))
             g_copy(t, half, g_a, 0).wait()
-            grad(t + 2, half, g_a, 0)
-            mm_t(t + 1, g_b, acc)
+            weave(mm_t(t + 1, g_b, acc), grad(t + 2, half, g_a, 0))
             tick(i)
             return carry
 
         lax.fori_loop(0, (full - 1) // 2, body, 0)
         g_copy(full - 2, half, g_b, 1).wait()
-        mm_t(full - 1, g_a, acc)
-        grad(full, half, g_b, 1, tail)
-        mm_t(full, g_b, acc, tail)
+        weave(mm_t(full - 1, g_a, acc), grad(full, half, g_b, 1, tail))
+        weave(mm_t(full, g_b, acc, tail), [])
         g_copy(full - 1, half, g_a, 0).wait()
         g_copy(full, half, g_b, 1, tail).wait()
 
@@ -385,7 +429,6 @@
         pltpu.make_async_copy(acc1.at[:, pl.ds(0, 8)], send_hbm, out_sem.at[0]),
         pltpu.make_async_copy(acc2.at[:, pl.ds(0, 8)], mine_hbm, out_sem.at[1]),
         pltpu.make_async_copy(acc2.at[:, pl.ds(8, 8)], part_hbm, out_sem.at[2]),
-        pltpu.make_async_copy(db_ref.at[0], db_hbm, out_sem.at[4]),
     ]
 
     def swap_tick(i):
@@ -398,7 +441,6 @@
     backward(0, acc2, swap_tick)
     outs[1].start()
     outs[2].start()
-    outs[3].start()
     for c in outs:
         c.wait()
     hb_out.wait()
@@ -408,7 +450,10 @@
         c.wait_send()
 
 
-def weight_kernel(gt_ref, hb_ref, out_ref):
+def weight_kernel(gt_ref, hb_ref, db_ref, out_ref, db_hbm, sem):
+    copy = pltpu.make_async_copy(db_ref.at[0], db_hbm, sem)
+    pl.when(pl.program_id(0) == 0)(copy.start)
+    pl.when(pl.program_id(0) == pl.num_programs(0) - 1)(copy.wait)
     out_ref[...] = dot(gt_ref[...], hb_ref[...]).astype(BF16)
 
 
@@ -435,13 +480,13 @@
             functools.partial(head_kernel, reg_weight),
             out_shape=(
                 jax.ShapeDtypeStruct((1, LANES), F32),
-                jax.ShapeDtypeStruct((vocab,), F32),
+                jax.ShapeDtypeStruct((1, vocab), F32),
                 jax.ShapeDtypeStruct((vocab, 2 * HALF), BF16),
                 jax.ShapeDtypeStruct((2, HALF, hidden), BF16),
                 block, block, block,
             ),
             in_specs=[vmem, vmem, vmem, vmem, hbm, hbm, hbm],
-            out_specs=(vmem, hbm, hbm, hbm, hbm, hbm, hbm),
+            out_specs=(vmem, vmem, hbm, hbm, hbm, hbm, hbm),
             scratch_shapes=[
                 pltpu.VMEM((vocab, hidden), BF16),
                 pltpu.VMEM((vocab, 2 * HALF), F32),
@@ -456,7 +501,6 @@
                 pltpu.VMEM((16, 8, hidden), F32),
                 pltpu.VMEM((64 * QUERIES, LANES), F32),
                 pltpu.VMEM((vocab, LANES), F32),
-                pltpu.VMEM((1, vocab), F32),
                 pltpu.VMEM((1, vocab), F32),
                 pltpu.VMEM((1, vocab), F32),
                 pltpu.VMEM((2, 8, LANES), F32),
@@ -485,30 +529,29 @@
         far = lax.ppermute(send.reshape(rows), 'tp', cross)
         near = lax.ppermute(part.reshape(rows), 'tp', swap)
         step = 800
-        d_weight = pl.pallas_call(
+        d_weight, d_bias = pl.pallas_call(
             weight_kernel,
             grid=(vocab // step,),
-            out_shape=jax.ShapeDtypeStruct((vocab, hidden), BF16),
+            out_shape=(jax.ShapeDtypeStruct((vocab, hidden), BF16), jax.ShapeDtypeStruct((vocab,), F32)),
             in_specs=[
                 pl.BlockSpec((step, 2 * HALF), lambda i: (i, 0)),
-                pl.BlockSpec((2 * HALF, hidden), lambda i: (0, 0)),
+                pl.BlockSpec((2 * HALF, hidden), lambda i: (0, 0), pipeline_mode=pl.Buffered(1)),
+                vmem,
             ],
-            out_specs=pl.BlockSpec((step, hidden), lambda i: (i, 0)),
+            out_specs=(pl.BlockSpec((step, hidden), lambda i: (i, 0)), hbm),
+            scratch_shapes=[dma],
             cost_estimate=pl.CostEstimate(
                 flops=2 * hidden * 2 * HALF * vocab, bytes_accessed=50_000_000, transcendentals=0
             ),
             compiler_params=pltpu.CompilerParams(vmem_limit_bytes=67_043_328),
             name='dweight',
-        )(gt, hb.reshape(2 * HALF, hidden))
+        )(gt, hb.reshape(2 * HALF, hidden), db)
         d_hidden = pl.pallas_call(
             finish_kernel,
-            grid=(4,),
             out_shape=jax.ShapeDtypeStruct(rows, BF16),
-            in_specs=[pl.BlockSpec((ROWS, hidden // 4), lambda i: (0, i))] * 3,
-            out_specs=pl.BlockSpec((ROWS, hidden // 4), lambda i: (0, i)),
             name='finish',
         )(mine.reshape(rows), near, far)
-        return loss[0, :1], d_weight.T, db, d_hidden.reshape(docs, doc_len, hidden)
+        return loss[0, :1], d_weight.T, d_bias, d_hidden.reshape(docs, doc_len, hidden)
 
     return jax.shard_map(
         local_step,

time: 117 us -> 106 us (0.906)
  Pallas kernels: 109 us -> 100 us
  local copies, waits for them, and re-layouts: 1.38 us -> 0 us
    pallas_call x1, Pallas kernels: 83.1 us -> 74.7 us  [local_step(): pl.pallas_call(functools.partial(head_kernel, reg_weight), out_shape=(jax...]
    unnamed x1 -> x0, local copies, waits for them, and re-layouts: 1.38 us -> none
  transfers between devices with their start and end apart: 2 -> 2, of which waited for: 1 -> 1; matrix products, arithmetic and copies ran while one was open for 0% -> 0% of each run, Pallas kernels for 19% -> 21%
where the time goes in v1:
time: 106 us
  Pallas kernels  100 us (94%)
  waiting for transfers between devices  3.03 us (3%)
  between operations  2.4 us (2%)
    pallas_call x1, Pallas kernels, local_step(): pl.pallas_call(functools.partial(head_kernel, reg_weight), out_shape=(jax...  74.7 us
    pallas_call x1, Pallas kernels, local_step(): pl.pallas_call(weight_kernel, grid=(vocab // step,), out_shape=(jax.Shape...  22.4 us
    ppermute x1, waiting for transfers between devices, local_step(): far = lax.ppermute(send.reshape(rows), 'tp', cross)  3.02 us
    pallas_call x1, Pallas kernels, local_step(): pl.pallas_call(finish_kernel, out_shape=jax.ShapeDtypeStruct(rows, BF16),...  2.96 us
  transfers between devices with their start and end apart: 2, of which 1 were waited for; matrix products, arithmetic and copies ran while one was open for 0% of the time, Pallas kernels for 21%

profile of v1, /device:TPU:0, one launch (start us, length us, event | category | flops | bytes accessed | tf_op | source)
XLA Modules:
  0.0 105.6 jit_solution(15031009193255797473)
XLA Ops:
  0.6 74.7 %head.1 = (f32[1,128]{1,0:T(1,128)}, f32[1,8000]{1,0:T(1,128)}, bf16[8000,512]{1,0:T(8,128)(2,1)}, bf16[2,256,2048]{2,1,0:T(8,128)(2,1)}, f32[16,8,2048]{2,1,0:T...) custom-call(bf16[128,2048]{1,0:T(8,128)(2,1)} %bitcast.13, s32[8,64]{1,0:T(8,128)} %ids_ref.1, s32[8,16]{1,0:T(8,128)} %mask_ref.1, ...), custom_call_target="tpu_custom_call" | custom-call | tf_op jit(solution)/shard_map/head/pallas_call | solution.py:479
  75.3 0.1 collective-permute-start
  75.5 0.0 collective-permute-start.1
  75.5 22.4 %dweight.1 = (bf16[8000,2048]{1,0:T(8,128)(2,1)}, f32[8000]{0:T(1024)}) custom-call(bf16[8000,512]{1,0:T(8,128)(2,1)} %get-tuple-element.14.gt_ref, bf16[512,2048]{1,0:T(8,128)(2,1)} %bitcast.16, f32[1,8000]{1,0:T(1,128)} %get-tuple-element.16.db_ref), custom_call_target="tpu_custom_call" | custom-call | flops 16777216000 | bytes 50000000 | tf_op jit(solution)/shard_map/dweight/pallas_call | solution.py:532
  97.9 0.0 collective-permute-done.part_ref
  97.9 3.0 %collective-permute-done.1.far_ref = f32[128,2048]{1,0:T(8,128)} collective-permute-done((f32[128,2048]{1,0:T(8,128)}, f32[128,2048]{1,0:T(8,128)}, u32[]{:S(2)}, u32[]{:S(2)}) %collective-permute-start.1) | collective-permute-done | bytes 1048608 | tf_op jit(solution)/shard_map/ppermute | solution.py:529
  100.9 3.0 %finish.1 = bf16[128,2048]{1,0:T(8,128)(2,1)} custom-call(f32[128,2048]{1,0:T(8,128)} %bitcast.12, f32[128,2048]{1,0:T(8,128)} %collective-permute-done.part_ref, f32[128,2048]{1,0:T(8,128)} %collective-permute-done.1.far_ref), custom_call_target="tpu_custom_call" | custom-call | tf_op jit(solution)/shard_map/finish/pallas_call | solution.py:549
Async XLA Ops:
  75.3 22.6 %collective-permute-start = (f32[128,2048]{1,0:T(8,128)}, f32[128,2048]{1,0:T(8,128)}, u32[]{:S(2)}, u32[]{:S(2)}) collective-permute-start(f32[128,2048]{1,0:T(8,128)} %bitcast.18), channel_id=1, source_target_pairs={{0,1},{1,0},{2,3},{3,2},{4,5},{5,4},{6,7},{7,6}} | collective-permute-start | bytes 3145736 | tf_op jit(solution)/shard_map/ppermute | solution.py:530
  75.5 25.5 %collective-permute-start.1 = (f32[128,2048]{1,0:T(8,128)}, f32[128,2048]{1,0:T(8,128)}, u32[]{:S(2)}, u32[]{:S(2)}) collective-permute-start(f32[128,2048]{1,0:T(8,128)} %bitcast.17), channel_id=1, source_target_pairs={{0,2},{1,3},{2,0},{3,1},{4,6},{5,7},{6,4},{7,5}} | collective-permute-start | bytes 3145736 | tf_op jit(solution)/shard_map/ppermute | solution.py:529

commit v2 on v1

--- a/solution.py
+++ b/solution.py
@@ -17,6 +17,7 @@
 ROWS = 128
 SUB = 64
 CHUNKS = 4
+EARLY = 256
 MM_ROWS = 256
 MM_COLS = 512
 QUERIES = 32
@@ -74,7 +75,7 @@
     loss_ref, db_ref, gt_hbm, hb_hbm, send_hbm, mine_hbm, part_hbm,
     wv, ybuf, hb, land, raw_a, raw_b, g_a, g_b, acc1, acc2, recv1,
     counts, bm, qw_ref, bias_ref, mask_row, ids_all, mask_all, pos_all, s_acc, reg_acc, inbox, ds6,
-    w_sem, hid_send, hid_recv, fwd_send, fwd_recv, pk_send, pk_recv, s_send, s_recv, acc_send, acc_recv, out_sem, g_sem,
+    w_sem, hid_send, hid_recv, fwd_send, fwd_recv, pk_send, pk_recv, s_send, s_recv, acc_send, acc_recv, far_send, far_recv, free_sem, out_sem, g_sem,
 ):
     vocab = wv.shape[0]
     hidden = wv.shape[1]
@@ -144,9 +145,8 @@
             stack = jnp.where(sub16[:, :size] == k, parts[k], stack)
         bm[at(t, 0, size)] = dot_tn(stack.astype(BF16), ones)
 
-    def bias_body(t, carry):
-        bias_columns(t, VT)
-        return carry
+    def bias_piece(t, size=VT):
+        return [functools.partial(bias_columns, t, size)]
 
     ids_all[me] = ids_ref[...]
     mask_all[me] = mask_ref[...]
@@ -187,8 +187,7 @@
 
     for c in rows_in:
         c.wait()
-    lax.fori_loop(0, full, bias_body, 0)
-    bias_columns(full, tail)
+    bias_columns(0, VT)
     near.wait_recv()
     place(0, (hid_ref, land.at[0]))
 
@@ -274,17 +273,17 @@
                 def _():
                     w_copy(full, tail).start()
                 w_copy(t + 1).wait()
-            weave(mm(t + 1, half, raw_b), ep(t, half, raw_a))
+            weave(mm(t + 1, half, raw_b), (bias_piece(t + 1) if first else []) + ep(t, half, raw_a))
             if first:
                 w_copy(t + 2).wait()
-            weave(mm(t + 2, half, raw_a), ep(t + 1, half, raw_b))
+            weave(mm(t + 2, half, raw_a), (bias_piece(t + 2) if first else []) + ep(t + 1, half, raw_b))
             tick(i)
             return carry
 
         lax.fori_loop(0, (full - 1) // 2, body, 0)
         if first:
             w_copy(full, tail).wait()
-        weave(mm(full, half, raw_b, tail), ep(full - 1, half, raw_a))
+        weave(mm(full, half, raw_b, tail), (bias_piece(full, tail) if first else []) + ep(full - 1, half, raw_a))
         weave([], ep(full, half, raw_b, tail))
 
     def relay_tick(i):
@@ -426,25 +425,36 @@
     swap = remote(acc1.at[:, pl.ds(8, 8)], recv1, acc_send, acc_recv, partner)
     swap.start()
     outs = [
-        pltpu.make_async_copy(acc1.at[:, pl.ds(0, 8)], send_hbm, out_sem.at[0]),
+        pltpu.make_async_copy(acc1.at[:, pl.ds(0, 8), pl.ds(EARLY, hidden - EARLY)], send_hbm, out_sem.at[0]),
         pltpu.make_async_copy(acc2.at[:, pl.ds(0, 8)], mine_hbm, out_sem.at[1]),
         pltpu.make_async_copy(acc2.at[:, pl.ds(8, 8)], part_hbm, out_sem.at[2]),
     ]
 
+    early = remote(acc1.at[:, pl.ds(0, 8), pl.ds(0, EARLY)], recv1.at[:, :, pl.ds(0, EARLY)], far_send, far_recv, other)
+
     def swap_tick(i):
-        @pl.when(i == 4)
+        @pl.when(i == 1)
         def _():
             swap.wait_recv()
             acc1[:, pl.ds(0, 8)] += recv1[...]
             outs[0].start()
+            pl.semaphore_signal(free_sem, inc=1, device_id={"tp": other}, device_id_type=MESH)
+
+        @pl.when(i == 2)
+        def _():
+            pl.semaphore_wait(free_sem, 1)
+            early.start()
 
     backward(0, acc2, swap_tick)
+    outs[2].start()
+    early.wait_recv()
+    acc2[:, pl.ds(0, 8), pl.ds(0, EARLY)] += recv1[:, :, pl.ds(0, EARLY)]
     outs[1].start()
-    outs[2].start()
     for c in outs:
         c.wait()
     hb_out.wait()
     swap.wait_send()
+    early.wait_send()
     near.wait_send()
     for c in pk_copies + far + relay + s_copies:
         c.wait_send()
@@ -458,9 +468,12 @@
 
 
 def finish_kernel(mine_ref, part_ref, far_ref, out_ref):
-    total = ((mine_ref[...] + part_ref[...]) + far_ref[...]).astype(BF16)
     r, k = iota((ROWS, ROWS), 0), iota((ROWS, ROWS), 1)
-    out_ref[...] = dot(one_hot(k == (r & 15) * 8 + (r >> 4)), total).astype(BF16)
+    perm = one_hot(k == (r & 15) * 8 + (r >> 4))
+    total = mine_ref[...] + part_ref[...]
+    early, late = pl.ds(0, EARLY), pl.ds(EARLY, total.shape[1] - EARLY)
+    out_ref[:, early] = dot(perm, total[:, :EARLY].astype(BF16)).astype(BF16)
+    out_ref[:, late] = dot(perm, (total[:, EARLY:] + far_ref[...]).astype(BF16)).astype(BF16)
 
 
 def solution(mesh):
@@ -483,7 +496,7 @@
                 jax.ShapeDtypeStruct((1, vocab), F32),
                 jax.ShapeDtypeStruct((vocab, 2 * HALF), BF16),
                 jax.ShapeDtypeStruct((2, HALF, hidden), BF16),
-                block, block, block,
+                jax.ShapeDtypeStruct((16, 8, hidden - EARLY), F32), block, block,
             ),
             in_specs=[vmem, vmem, vmem, vmem, hbm, hbm, hbm],
             out_specs=(vmem, vmem, hbm, hbm, hbm, hbm, hbm),
@@ -512,7 +525,7 @@
                 pltpu.VMEM((4, 40, LANES), F32),
                 pltpu.VMEM((192, HALF), BF16),
                 dma((tiles,)), dma((CHUNKS + 1,)), dma((CHUNKS + 1,)), dma((CHUNKS,)), dma((CHUNKS,)),
-                dma((9,)), dma((9,)), dma((3,)), dma((3,)), dma, dma, dma((5,)), dma((2,)),
+                dma((9,)), dma((9,)), dma((3,)), dma((3,)), dma, dma, dma, dma, pltpu.SemaphoreType.REGULAR, dma((5,)), dma((2,)),
             ],
             compiler_params=pltpu.CompilerParams(
                 collective_id=0, has_side_effects=True, vmem_limit_bytes=67_043_328
@@ -526,7 +539,7 @@
         cross = [(k, (k + 2) % 4) for k in range(4)]
         swap = [(k, k ^ 1) for k in range(4)]
         rows = (docs * doc_len, hidden)
-        far = lax.ppermute(send.reshape(rows), 'tp', cross)
+        far = lax.ppermute(send.reshape(rows[0], hidden - EARLY), 'tp', cross)
         near = lax.ppermute(part.reshape(rows), 'tp', swap)
         step = 800
         d_weight, d_bias = pl.pallas_call(

time: 106 us -> 99.8 us (0.942)
  Pallas kernels: 100 us -> 96.5 us
  waiting for transfers between devices: 3.03 us -> 0.01 us
    pallas_call x1, Pallas kernels: 74.7 us -> 71.2 us  [local_step(): pl.pallas_call(functools.partial(head_kernel, reg_weight), out_shape=(jax...]
    ppermute x1, waiting for transfers between devices: 3.02 us -> 0.01 us  [local_step(): far = lax.ppermute(send.reshape(rows[0], hidden - EARLY), 'tp', cross)]
  transfers between devices with their start and end apart: 2 -> 2, of which waited for: 1 -> 0; matrix products, arithmetic and copies ran while one was open for 0% -> 0% of each run, Pallas kernels for 21% -> 23%
where the time goes in v2:
time: 99.8 us; the launch traced here: 99.6 us
  Pallas kernels  96.5 us (97%)
  between operations  2.42 us (2%)
    pallas_call x1, Pallas kernels, local_step(): pl.pallas_call(functools.partial(head_kernel, reg_weight), out_shape=(jax...  71.2 us
    pallas_call x1, Pallas kernels, local_step(): pl.pallas_call(weight_kernel, grid=(vocab // step,), out_shape=(jax.Shape...  22.4 us
    pallas_call x1, Pallas kernels, local_step(): pl.pallas_call(finish_kernel, out_shape=jax.ShapeDtypeStruct(rows, BF16),...  2.92 us
  transfers between devices with their start and end apart: 2, of which 0 were waited for; matrix products, arithmetic and copies ran while one was open for 0% of the time, Pallas kernels for 23%

profile of v2, /device:TPU:0, one launch (start us, length us, event | category | flops | bytes accessed | tf_op | source)
XLA Modules:
  0.0 99.6 jit_solution(18280337247338463473)
XLA Ops:
  0.6 71.2 %head.1 = (f32[1,128]{1,0:T(1,128)}, f32[1,8000]{1,0:T(1,128)}, bf16[8000,512]{1,0:T(8,128)(2,1)}, bf16[2,256,2048]{2,1,0:T(8,128)(2,1)}, f32[16,8,1792]{2,1,0:T...) custom-call(bf16[128,2048]{1,0:T(8,128)(2,1)} %bitcast.13, s32[8,64]{1,0:T(8,128)} %ids_ref.1, s32[8,16]{1,0:T(8,128)} %mask_ref.1, ...), custom_call_target="tpu_custom_call" | custom-call | tf_op jit(solution)/shard_map/head/pallas_call | solution.py:492
  71.9 0.6 collective-permute-start.1
  72.5 0.0 collective-permute-start
  72.5 22.4 %dweight.1 = (bf16[8000,2048]{1,0:T(8,128)(2,1)}, f32[8000]{0:T(1024)}) custom-call(bf16[8000,512]{1,0:T(8,128)(2,1)} %get-tuple-element.14.gt_ref, bf16[512,2048]{1,0:T(8,128)(2,1)} %bitcast.16, f32[1,8000]{1,0:T(1,128)} %get-tuple-element.16.db_ref), custom_call_target="tpu_custom_call" | custom-call | flops 16777216000 | bytes 50000000 | tf_op jit(solution)/shard_map/dweight/pallas_call | solution.py:545
  94.9 0.0 collective-permute-done.1.far_ref
  94.9 0.0 collective-permute-done.part_ref
  94.9 2.9 %finish.1 = bf16[128,2048]{1,0:T(8,128)(2,1)} custom-call(f32[128,2048]{1,0:T(8,128)} %bitcast.12, f32[128,2048]{1,0:T(8,128)} %collective-permute-done.part_ref, f32[128,1792]{1,0:T(8,128)} %collective-permute-done.1.far_ref), custom_call_target="tpu_custom_call" | custom-call | tf_op jit(solution)/shard_map/finish/pallas_call | solution.py:562
Async XLA Ops:
  71.9 23.1 %collective-permute-start.1 = (f32[128,1792]{1,0:T(8,128)}, f32[128,1792]{1,0:T(8,128)}, u32[]{:S(2)}, u32[]{:S(2)}) collective-permute-start(f32[128,1792]{1,0:T(8,128)} %bitcast.18), channel_id=1, source_target_pairs={{0,2},{1,3},{2,0},{3,1},{4,6},{5,7},{6,4},{7,5}} | collective-permute-start | bytes 2752520 | tf_op jit(solution)/shard_map/ppermute | solution.py:542
  72.5 22.4 %collective-permute-start = (f32[128,2048]{1,0:T(8,128)}, f32[128,2048]{1,0:T(8,128)}, u32[]{:S(2)}, u32[]{:S(2)}) collective-permute-start(f32[128,2048]{1,0:T(8,128)} %bitcast.17), channel_id=1, source_target_pairs={{0,1},{1,0},{2,3},{3,2},{4,5},{5,4},{6,7},{7,6}} | collective-permute-start | bytes 3145736 | tf_op jit(solution)/shard_map/ppermute | solution.py:543

commit v3 on v2

--- a/solution.py
+++ b/solution.py
@@ -347,14 +347,16 @@
             buf.at[pl.ds(0, size)], gt_hbm.at[at(t, 0, size), pl.ds(half * HALF, HALF)], g_sem.at[k]
         )
 
-    def grad(t, half, buf, k, size=VT):
-        def setup(off):
+    def setup(t, half, size=VT):
+        def piece(off):
             def run():
                 depth = min(HALF, size - off)
                 hi, mid, lo = split3(query_rep(t, off, depth))
                 raw_a[pl.ds(off, depth)] = dot_tn(jnp.concatenate([hi, hi, mid, hi, mid, lo], axis=0), ds6[...])
             return run
-
+        return [piece(off) for off in range(0, size, HALF)] if half == 1 else []
+
+    def grad(t, half, buf, k, size=VT):
         def rows_piece(r):
             def run():
                 rows = pl.ds(r * SUB, SUB)
@@ -383,12 +385,7 @@
                 else:
                     db_ref[:, cols(t, off, width)] += row
 
-        out = []
-        for off in range(0, size, HALF):
-            if half == 1:
-                out.append(setup(off))
-            out += [rows_piece(r) for r in range(off // SUB, min(off + HALF, size) // SUB)]
-        return out + [finish]
+        return [rows_piece(r) for r in range(size // SUB)] + [finish]
 
     def mm_t(t, buf, acc, size=VT):
         def piece(n):
@@ -400,7 +397,10 @@
 
     def backward(half, acc, tick):
         acc[...] = jnp.zeros_like(acc)
-        weave([], grad(0, half, g_a, 0))
+        weave([], setup(0, half) + grad(0, half, g_a, 0) + setup(1, half))
+
+        def setup_next(t):
+            return setup(jnp.minimum(t, full - 1), half)
 
         def body(i, carry):
             t = 2 * i
@@ -408,15 +408,15 @@
             @pl.when(i > 0)
             def _():
                 g_copy(t - 1, half, g_b, 1).wait()
-            weave(mm_t(t, g_a, acc), grad(t + 1, half, g_b, 1))
+            weave(mm_t(t, g_a, acc), grad(t + 1, half, g_b, 1) + setup(t + 2, half))
             g_copy(t, half, g_a, 0).wait()
-            weave(mm_t(t + 1, g_b, acc), grad(t + 2, half, g_a, 0))
+            weave(mm_t(t + 1, g_b, acc), grad(t + 2, half, g_a, 0) + setup_next(t + 3))
             tick(i)
             return carry
 
         lax.fori_loop(0, (full - 1) // 2, body, 0)
         g_copy(full - 2, half, g_b, 1).wait()
-        weave(mm_t(full - 1, g_a, acc), grad(full, half, g_b, 1, tail))
+        weave(mm_t(full - 1, g_a, acc), setup(full, half, tail) + grad(full, half, g_b, 1, tail))
         weave(mm_t(full, g_b, acc, tail), [])
         g_copy(full - 1, half, g_a, 0).wait()
         g_copy(full, half, g_b, 1, tail).wait()

time: 99.8 us -> 99.4 us (level)
  no operation moved by 1% of the time
where the time goes in v3:
time: 99.4 us; the launch traced here: 99.2 us
  Pallas kernels  96.2 us (97%)
  between operations  2.42 us (2%)
    pallas_call x1, Pallas kernels, local_step(): pl.pallas_call(functools.partial(head_kernel, reg_weight), out_shape=(jax...  70.8 us
    pallas_call x1, Pallas kernels, local_step(): pl.pallas_call(weight_kernel, grid=(vocab // step,), out_shape=(jax.Shape...  22.4 us
    pallas_call x1, Pallas kernels, local_step(): pl.pallas_call(finish_kernel, out_shape=jax.ShapeDtypeStruct(rows, BF16),...  2.92 us
  transfers between devices with their start and end apart: 2, of which 0 were waited for; matrix products, arithmetic and copies ran while one was open for 0% of the time, Pallas kernels for 23%

profile of v3, /device:TPU:0, one launch (start us, length us, event | category | flops | bytes accessed | tf_op | source)
XLA Modules:
  0.0 99.2 jit_solution(9437698490269204837)
XLA Ops:
  0.6 70.8 %head.1 = (f32[1,128]{1,0:T(1,128)}, f32[1,8000]{1,0:T(1,128)}, bf16[8000,512]{1,0:T(8,128)(2,1)}, bf16[2,256,2048]{2,1,0:T(8,128)(2,1)}, f32[16,8,1792]{2,1,0:T...) custom-call(bf16[128,2048]{1,0:T(8,128)(2,1)} %bitcast.13, s32[8,64]{1,0:T(8,128)} %ids_ref.1, s32[8,16]{1,0:T(8,128)} %mask_ref.1, ...), custom_call_target="tpu_custom_call" | custom-call | tf_op jit(solution)/shard_map/head/pallas_call | solution.py:492
  71.5 0.6 collective-permute-start.1
  72.1 0.0 collective-permute-start
  72.1 22.4 %dweight.1 = (bf16[8000,2048]{1,0:T(8,128)(2,1)}, f32[8000]{0:T(1024)}) custom-call(bf16[8000,512]{1,0:T(8,128)(2,1)} %get-tuple-element.14.gt_ref, bf16[512,2048]{1,0:T(8,128)(2,1)} %bitcast.16, f32[1,8000]{1,0:T(1,128)} %get-tuple-element.16.db_ref), custom_call_target="tpu_custom_call" | custom-call | flops 16777216000 | bytes 50000000 | tf_op jit(solution)/shard_map/dweight/pallas_call | solution.py:545
  94.5 0.0 collective-permute-done.1.far_ref
  94.5 0.0 collective-permute-done.part_ref
  94.5 2.9 %finish.1 = bf16[128,2048]{1,0:T(8,128)(2,1)} custom-call(f32[128,2048]{1,0:T(8,128)} %bitcast.12, f32[128,2048]{1,0:T(8,128)} %collective-permute-done.part_ref, f32[128,1792]{1,0:T(8,128)} %collective-permute-done.1.far_ref), custom_call_target="tpu_custom_call" | custom-call | tf_op jit(solution)/shard_map/finish/pallas_call | solution.py:562
Async XLA Ops:
  71.5 23.1 %collective-permute-start.1 = (f32[128,1792]{1,0:T(8,128)}, f32[128,1792]{1,0:T(8,128)}, u32[]{:S(2)}, u32[]{:S(2)}) collective-permute-start(f32[128,1792]{1,0:T(8,128)} %bitcast.18), channel_id=1, source_target_pairs={{0,2},{1,3},{2,0},{3,1},{4,6},{5,7},{6,4},{7,5}} | collective-permute-start | bytes 2752520 | tf_op jit(solution)/shard_map/ppermute | solution.py:542
  72.1 22.4 %collective-permute-start = (f32[128,2048]{1,0:T(8,128)}, f32[128,2048]{1,0:T(8,128)}, u32[]{:S(2)}, u32[]{:S(2)}) collective-permute-start(f32[128,2048]{1,0:T(8,128)} %bitcast.17), channel_id=1, source_target_pairs={{0,1},{1,0},{2,3},{3,2},{4,5},{5,4},{6,7},{7,6}} | collective-permute-start | bytes 3145736 | tf_op jit(solution)/shard_map/ppermute | solution.py:543
